TPU v7x, 32 devices: a whole 2x2x4 slice. The times are simulated.
32 devices in a mesh: trial: 2 (over core), bank: 4 (over y, x), zero: 4 (over z).
Axes of the slice: x: 2, y: 2, z: 4, core: 2. Of those that a mesh axis runs over, the one named last changes fastest.
Arguments:
- w_gate: float32 [128, 2048, 1024], P(('trial', 'bank'), 'zero'), parts along dimension 0, may hold values from -0.1875 to 0.1875
- w_up: float32 [128, 2048, 1024], P(('trial', 'bank'), 'zero'), parts along dimension 0, may hold values from -0.1875 to 0.1875
- router_weight: float32 [4096, 64], P(('trial', 'zero'), 'bank'), parts along dimension 0, may hold values from -0.125 to 0.125
- router_gain: float32 [4096], P(('trial', 'zero')), parts along dimension 0, may hold values from 0.25 to 1.75
Outputs:
- serve_gate: bfloat16 [128, 2048, 1024], P(('trial', 'bank'), None, 'zero'), parts along dimension 0
- serve_up: bfloat16 [128, 2048, 1024], P(('trial', 'bank'), None, 'zero'), parts along dimension 0
- scale_gate: float32 [128, 1024], P(('trial', 'bank'), 'zero'), parts along dimension 0
- scale_up: float32 [128, 1024], P(('trial', 'bank'), 'zero'), parts along dimension 0
- serve_router: bfloat16 [4096, 64], P('trial'), parts along dimension 0
There are 2 independent parts, one for each index of `trial`. A program takes and returns all parts, laid end to end along the dimension named above; each array names one. Nothing has to cross between parts.
All inputs are finite; a program needn't handle non-finite values. Where the computation divides by a largest or mean magnitude, that divisor is 1e-20 or more.
Results may differ from a plain program's by a relative error of at most 0.001.
Values may be sent and summed in bfloat16 or wider, within the bound.
A program may use at most 192 MiB of HBM per device.

v0:
```python
import jax
import jax.numpy as jnp
from jax import lax
from jax.sharding import PartitionSpec as P

D_MODEL = 2048


def local(w_gate, w_up, router_weight, router_gain):
    total_gate, total_up = lax.psum(
        (jnp.sum(jnp.abs(w_gate), axis=1), jnp.sum(jnp.abs(w_up), axis=1)), "zero"
    )
    scale_gate = total_gate / D_MODEL
    scale_up = total_up / D_MODEL
    narrow_gate, narrow_up = (
        (w_gate / jnp.expand_dims(scale_gate, 1)).astype(jnp.bfloat16),
        (w_up / jnp.expand_dims(scale_up, 1)).astype(jnp.bfloat16),
    )
    serve_gate, serve_up = (
        lax.all_to_all(narrow_gate, "zero", split_axis=2, concat_axis=1, tiled=True),
        lax.all_to_all(narrow_up, "zero", split_axis=2, concat_axis=1, tiled=True),
    )
    scale_gate = lax.dynamic_slice_in_dim(
        scale_gate, lax.axis_index("zero") * serve_gate.shape[2], serve_gate.shape[2], axis=1
    )
    scale_up = lax.dynamic_slice_in_dim(
        scale_up, lax.axis_index("zero") * serve_up.shape[2], serve_up.shape[2], axis=1
    )
    part_router = (router_weight * router_gain[:, None]).astype(jnp.bfloat16)
    row_router = lax.all_gather(part_router, "zero", axis=0, tiled=True)
    serve_router = lax.all_gather(row_router, "bank", axis=1, tiled=True)
    return (serve_gate, serve_up, scale_gate, scale_up, serve_router)


def solution(mesh):
    placed = (
        P(("trial", "bank"), "zero", None),
        P(("trial", "bank"), "zero", None),
        P(("trial", "zero"), "bank"),
        P(("trial", "zero")),
    )
    return jax.shard_map(
        local,
        mesh=mesh,
        in_specs=placed,
        out_specs=(
            P(("trial", "bank"), None, "zero"),
            P(("trial", "bank"), None, "zero"),
            P(("trial", "bank"), "zero"),
            P(("trial", "bank"), "zero"),
            P("trial", None),
        ),
        check_vma=False,
    )
```

profile of v0, /device:TPU:0, one launch (start us, length us, event | category | flops | bytes accessed | tf_op | source)
XLA Modules:
  0.0 899.1 jit_solution(11479732921372934390)
XLA Ops:
  7.2 0.0 all-reduce.3.cloned.1.call-start
  7.2 22.1 %abs_reduce_fusion = (f32[16,1024]{1,0:T(8,128)}, f32[16,1024]{1,0:T(8,128)}) fusion(f32[16,512,1024]{2,1,0:T(8,128)} %param.5, f32[16,512,1024]{2,1,0:T(8,128)} %param.4), kind=kLoop, calls=%fused_computation.1 | loop fusion | flops 33521664 | bytes 67239936 | tf_op jit(solution)/shard_map/reduce_sum | solution.py:11
  29.3 0.0 all-reduce.3.cloned.1.call-update
  29.3 34.3 %copy.15 = f32[16,512,1024]{1,0,2:T(8,128)} copy(f32[16,512,1024]{2,1,0:T(8,128)} %param.5) | data formatting | bytes 67108864 | tf_op args[1]
  63.6 3.3 all-reduce.3.cloned.1.call-done
  66.9 0.8 broadcast_multiply_fusion
  67.8 0.2 copy.14
  68.0 17.7 %divide_convert_fusion = bf16[16,512,1024]{1,0,2:T(8,128)(2,1)} fusion(f32[16,512,1024]{1,0,2:T(8,128)} %copy.15, f32[16,1024]{0,1:T(8,128)S(1)} %copy.14), kind=kLoop, calls=%fused_computation | loop fusion | flops 16777216 | bytes 50397184 | tf_op jit(solution)/shard_map/convert_element_type | solution.py:17
  85.6 7.1 all-to-all-start.1
  92.7 0.0 copy-start
  92.7 34.2 %copy.12 = f32[16,512,1024]{1,0,2:T(8,128)} copy(f32[16,512,1024]{2,1,0:T(8,128)} %param.4) | data formatting | bytes 67108864 | tf_op args[0]
  126.9 0.0 copy-done
  126.9 0.2 copy.11
  127.1 0.0 copy-start.1
  127.1 0.0 copy-start.2
  127.1 17.7 %divide_convert_fusion.1 = bf16[16,512,1024]{1,0,2:T(8,128)(2,1)} fusion(f32[16,512,1024]{1,0,2:T(8,128)} %copy.12, f32[16,1024]{0,1:T(8,128)S(1)} %copy.11), kind=kLoop, calls=%fused_computation.2 | loop fusion | flops 16777216 | bytes 50397184 | tf_op jit(solution)/shard_map/convert_element_type | solution.py:16
  144.8 308.9 %all-to-all-done.1 = bf16[16,512,1024]{1,0,2:T(8,128)(2,1)} async-done(((bf16[16,512,1024]{1,0,2:T(8,128)(2,1)}), bf16[16,512,1024]{1,0,2:T(8,128)(2,1)}, u32[]{:S(2)}, u32[]{:S(2)}) %all-to-all-start.1) | async-done | bytes 16777248 | tf_op jit(solution)/shard_map/all_to_all | solution.py:21
  453.7 7.0 all-to-all-start
  460.7 0.0 copy-done.1
  460.7 0.0 copy-done.2
  460.8 367.8 %all_gather.6 = bf16[2048,16]{0,1:T(8,128)(2,1)S(1)} all-gather(bf16[512,16]{0,1:T(8,128)(2,1)S(1)} %multiply_convert_fusion), channel_id=1, replica_groups=mesh['trial'=2,'bank'=4,'zero'=4] {'zero'}, dimensions={0}, use_global_device_ids=true | all-gather | bytes 81920 | tf_op jit(solution)/shard_map/all_gather | solution.py:30
  828.5 9.5 %all_gather.7 = bf16[2048,64]{0,1:T(8,128)(2,1)S(1)} all-gather(bf16[2048,16]{0,1:T(8,128)(2,1)S(1)} %all_gather.6), channel_id=1, replica_groups=mesh['trial'=2,'bank'=4,'zero'=4] {'bank'}, dimensions={1}, use_global_device_ids=true | all-gather | bytes 327680 | tf_op jit(solution)/shard_map/all_gather | solution.py:31
  838.0 0.6 constant_dynamic-slice_fusion
  838.6 0.6 constant_dynamic-slice_fusion.1
  839.2 26.2 %copy.16 = bf16[16,4,512,256]{3,2,1,0:T(8,128)(2,1)} copy(bf16[16,4,512,256]{2,0,3,1:T(8,128)(2,1)} %bitcast.4) | data formatting | bytes 33554432 | tf_op jit(solution)/shard_map/all_to_all | solution.py:21
  865.4 0.0 all-to-all-done
  865.4 26.2 %copy.13 = bf16[16,4,512,256]{3,2,1,0:T(8,128)(2,1)} copy(bf16[16,4,512,256]{2,0,3,1:T(8,128)(2,1)} %bitcast.1) | data formatting | bytes 33554432 | tf_op jit(solution)/shard_map/all_to_all | solution.py:20
  891.6 0.7 copy.20
  (2 shorter events, 0.0 us)
Async XLA Ops:
  7.2 59.7 %all-reduce.3.cloned.1.call-start = ((), (), s32[]{:S(2)}) async-start(), calls=%async_computation.2 | async-start | bytes 262144 | tf_op jit(solution)/shard_map/psum | solution.py:10
  85.6 368.1 %all-to-all-start.1 = ((bf16[16,512,1024]{1,0,2:T(8,128)(2,1)}), bf16[16,512,1024]{1,0,2:T(8,128)(2,1)}, u32[]{:S(2)}, u32[]{:S(2)}) async-start(bf16[16,512,1024]{1,0,2:T(8,128)(2,1)} %divide_convert_fusion), calls=%async_computation.1 | async-start | bytes 33554432 | tf_op jit(solution)/shard_map/all_to_all | solution.py:21
  92.7 34.2 %copy-start = (f32[16,1024]{1,0:T(8,128)S(1)}, f32[16,1024]{1,0:T(8,128)}, u32[]{:S(2)}) copy-start(f32[16,1024]{1,0:T(8,128)} %get-tuple-element.5) | copy-start | bytes 196612
  127.1 333.6 %copy-start.1 = (f32[512,16]{0,1:T(8,128)S(1)}, f32[512,16]{0,1:T(8,128)}, u32[]{:S(2)}) copy-start(f32[512,16]{0,1:T(8,128)} %param.6) | copy-start | bytes 98308
  127.1 333.6 %copy-start.2 = (f32[512]{0:T(512)S(1)}, f32[512]{0:T(512)}, u32[]{:S(2)}) copy-start(f32[512]{0:T(512)} %param.7) | copy-start | bytes 6148
  453.7 411.7 %all-to-all-start = ((bf16[16,512,1024]{1,0,2:T(8,128)(2,1)}), bf16[16,512,1024]{1,0,2:T(8,128)(2,1)}, u32[]{:S(2)}, u32[]{:S(2)}) async-start(bf16[16,512,1024]{1,0,2:T(8,128)(2,1)} %divide_convert_fusion.1), calls=%async_computation | async-start | bytes 33554432 | tf_op jit(solution)/shard_map/all_to_all | solution.py:20
Sparse Core Ops, SparseCore 0:
  29.4 37.4 all-reduce.2
where the time goes:
time: 902 us; the launch traced here: 899 us
  blocking collectives  377 us (42%)
  waiting for transfers between devices  312 us (35%)
  local copies, waits for them, and re-layouts  123 us (14%)
  other arithmetic  58.3 us (6%)
  starting transfers between devices  14.1 us (2%)
  between operations  14.1 us (2%)
    all_gather x1, blocking collectives, local(): row_router = lax.all_gather(part_router, 'zero', axis=0, tiled=True)  368 us
    all_to_all x1, waiting for transfers between devices, local(): lax.all_to_all(narrow_up, 'zero', split_axis=2, concat_axis=1, tiled=True)  309 us
    unnamed x9, local copies, waits for them, and re-layouts  69.1 us
    all_to_all x1, local copies, waits for them, and re-layouts, local(): lax.all_to_all(narrow_gate, 'zero', split_axis=2, concat_axis=1, tiled=True)  26.2 us
    all_to_all x1, local copies, waits for them, and re-layouts, local(): lax.all_to_all(narrow_up, 'zero', split_axis=2, concat_axis=1, tiled=True)  26.2 us
    reduce_sum x1, other arithmetic, local(): jnp.sum(jnp.abs(w_up), axis=1)  22.1 us
  transfers between devices with their start and end apart: 3, of which 2 were waited for; matrix products, arithmetic and copies ran while one was open for 13% of the time, Pallas kernels for 0%

commit v1 on v0

--- a/solution.py
+++ b/solution.py
@@ -27,7 +27,9 @@
         scale_up, lax.axis_index("zero") * serve_up.shape[2], serve_up.shape[2], axis=1
     )
     part_router = (router_weight * router_gain[:, None]).astype(jnp.bfloat16)
-    row_router = lax.all_gather(part_router, "zero", axis=0, tiled=True)
+    row_router = jnp.concatenate(
+        lax.all_to_all(jnp.stack([part_router] * lax.axis_size("zero")), "zero", 0, 0), axis=0
+    )
     serve_router = lax.all_gather(row_router, "bank", axis=1, tiled=True)
     return (serve_gate, serve_up, scale_gate, scale_up, serve_router)
 

time: 902 us -> 865 us (0.959)
  blocking collectives: 377 us -> 8.98 us
  waiting for transfers between devices: 312 us -> 637 us
    all_gather x1 -> x0, blocking collectives: 368 us -> none  [local(): row_router = lax.all_gather(part_router, 'zero', axis=0, tiled=True)]
    all_to_all x1, waiting for transfers between devices: 0.01 us -> 326 us  [local(): lax.all_to_all(narrow_gate, 'zero', split_axis=2, concat_axis=1, tiled=True)]
  transfers between devices with their start and end apart: 3 -> 4, of which waited for: 2 -> 2; matrix products, arithmetic and copies ran while one was open for 13% -> 15% of each run, Pallas kernels for 0% -> 0%
where the time goes in v1:
time: 865 us; the launch traced here: 862 us
  waiting for transfers between devices  637 us (74%)
  local copies, waits for them, and re-layouts  124 us (14%)
  other arithmetic  58.3 us (7%)
  starting transfers between devices  20.4 us (2%)
  between operations  14.1 us (2%)
  blocking collectives  8.98 us (1%)
    all_to_all x1, waiting for transfers between devices, local(): lax.all_to_all(narrow_gate, 'zero', split_axis=2, concat_axis=1, tiled=True)  326 us
    all_to_all x1, waiting for transfers between devices, local(): lax.all_to_all(narrow_up, 'zero', split_axis=2, concat_axis=1, tiled=True)  311 us
    unnamed x9, local copies, waits for them, and re-layouts  69.1 us
    all_to_all x1, local copies, waits for them, and re-layouts, local(): lax.all_to_all(narrow_gate, 'zero', split_axis=2, concat_axis=1, tiled=True)  26.2 us
    all_to_all x1, local copies, waits for them, and re-layouts, local(): lax.all_to_all(narrow_up, 'zero', split_axis=2, concat_axis=1, tiled=True)  26.2 us
    reduce_sum x1, other arithmetic, local(): jnp.sum(jnp.abs(w_up), axis=1)  22.1 us
    convert_element_type x1, other arithmetic, local(): (w_up / jnp.expand_dims(scale_up, 1)).astype(jnp.bfloat16)  17.7 us
    convert_element_type x1, other arithmetic, local(): (w_gate / jnp.expand_dims(scale_gate, 1)).astype(jnp.bfloat16)  17.7 us
  transfers between devices with their start and end apart: 4, of which 2 were waited for; matrix products, arithmetic and copies ran while one was open for 15% of the time, Pallas kernels for 0%

profile of v1, /device:TPU:0, one launch (start us, length us, event | category | flops | bytes accessed | tf_op | source)
XLA Modules:
  0.0 862.3 jit_solution(10664500630655038486)
XLA Ops:
  7.2 0.0 copy-start.1
  7.2 0.0 copy-start.2
  7.2 0.0 all-reduce.3.cloned.1.call-start
  7.2 22.1 %abs_reduce_fusion = (f32[16,1024]{1,0:T(8,128)}, f32[16,1024]{1,0:T(8,128)}) fusion(f32[16,512,1024]{2,1,0:T(8,128)} %param.5, f32[16,512,1024]{2,1,0:T(8,128)} %param.4), kind=kLoop, calls=%fused_computation.1 | loop fusion | flops 33521664 | bytes 67239936 | tf_op jit(solution)/shard_map/reduce_sum | solution.py:11
  29.3 0.0 all-reduce.3.cloned.1.call-update
  29.3 0.0 copy-done.1
  29.4 0.0 copy-done.2
  29.4 0.6 stack.2
  30.0 6.3 all-to-all-start.2
  36.4 34.3 %copy.21 = f32[16,512,1024]{1,0,2:T(8,128)} copy(f32[16,512,1024]{2,1,0:T(8,128)} %param.5) | data formatting | bytes 67108864 | tf_op args[1]
  70.6 0.0 all-reduce.3.cloned.1.call-done
  70.6 0.8 broadcast_multiply_fusion
  71.5 0.2 copy.20
  71.7 17.7 %divide_convert_fusion = bf16[16,512,1024]{1,0,2:T(8,128)(2,1)} fusion(f32[16,512,1024]{1,0,2:T(8,128)} %copy.21, f32[16,1024]{0,1:T(8,128)S(1)} %copy.20), kind=kLoop, calls=%fused_computation | loop fusion | flops 16777216 | bytes 50397184 | tf_op jit(solution)/shard_map/convert_element_type | solution.py:17
  89.3 0.0 all-to-all-done.2
  89.3 7.1 all-to-all-start.1
  96.4 0.0 copy-start
  96.4 34.1 %copy.18 = f32[16,512,1024]{1,0,2:T(8,128)} copy(f32[16,512,1024]{2,1,0:T(8,128)} %param.4) | data formatting | bytes 67108864 | tf_op args[0]
  130.6 0.0 copy-done
  130.6 0.2 copy.17
  130.8 17.7 %divide_convert_fusion.1 = bf16[16,512,1024]{1,0,2:T(8,128)(2,1)} fusion(f32[16,512,1024]{1,0,2:T(8,128)} %copy.18, f32[16,1024]{0,1:T(8,128)S(1)} %copy.17), kind=kLoop, calls=%fused_computation.2 | loop fusion | flops 16777216 | bytes 50397184 | tf_op jit(solution)/shard_map/convert_element_type | solution.py:16
  148.5 310.7 %all-to-all-done.1 = bf16[16,512,1024]{1,0,2:T(8,128)(2,1)} async-done(((bf16[16,512,1024]{1,0,2:T(8,128)(2,1)}), bf16[16,512,1024]{1,0,2:T(8,128)(2,1)}, u32[]{:S(2)}, u32[]{:S(2)}) %all-to-all-start.1) | async-done | bytes 16777248 | tf_op jit(solution)/shard_map/all_to_all | solution.py:21
  459.2 7.0 all-to-all-start
  466.2 9.0 %all_gather.3 = bf16[2048,64]{0,1:T(8,128)(2,1)S(1)} all-gather(bf16[2048,16]{0,1:T(8,128)(2,1)S(1)} %bitcast.12), channel_id=1, replica_groups=mesh['trial'=2,'bank'=4,'zero'=4] {'bank'}, dimensions={1}, use_global_device_ids=true | all-gather | bytes 327680 | tf_op jit(solution)/shard_map/all_gather | solution.py:33
  475.1 0.6 constant_dynamic-slice_fusion
  475.8 0.6 constant_dynamic-slice_fusion.1
  476.4 26.2 %copy.22 = bf16[16,4,512,256]{3,2,1,0:T(8,128)(2,1)} copy(bf16[16,4,512,256]{2,0,3,1:T(8,128)(2,1)} %bitcast.4) | data formatting | bytes 33554432 | tf_op jit(solution)/shard_map/all_to_all | solution.py:21
  502.5 326.0 %all-to-all-done = bf16[16,512,1024]{1,0,2:T(8,128)(2,1)} async-done(((bf16[16,512,1024]{1,0,2:T(8,128)(2,1)}), bf16[16,512,1024]{1,0,2:T(8,128)(2,1)}, u32[]{:S(2)}, u32[]{:S(2)}) %all-to-all-start) | async-done | bytes 16777248 | tf_op jit(solution)/shard_map/all_to_all | solution.py:20
  828.6 26.2 %copy.19 = bf16[16,4,512,256]{3,2,1,0:T(8,128)(2,1)} copy(bf16[16,4,512,256]{2,0,3,1:T(8,128)(2,1)} %bitcast.1) | data formatting | bytes 33554432 | tf_op jit(solution)/shard_map/all_to_all | solution.py:20
  854.7 0.7 copy.28
  (3 shorter events, 0.0 us)
Async XLA Ops:
  7.2 22.2 %copy-start.1 = (f32[512,16]{0,1:T(8,128)S(1)}, f32[512,16]{0,1:T(8,128)}, u32[]{:S(2)}) copy-start(f32[512,16]{0,1:T(8,128)} %param.6) | copy-start | bytes 98308
  7.2 22.2 %copy-start.2 = (f32[512]{0:T(512)S(1)}, f32[512]{0:T(512)}, u32[]{:S(2)}) copy-start(f32[512]{0:T(512)} %param.7) | copy-start | bytes 6148
  7.2 63.4 %all-reduce.3.cloned.1.call-start = ((), (), s32[]{:S(2)}) async-start(), calls=%async_computation.3 | async-start | bytes 262144 | tf_op jit(solution)/shard_map/psum | solution.py:10
  30.0 59.3 %all-to-all-start.2 = ((bf16[4,512,16]{1,2,0:T(8,128)(2,1)}), bf16[4,512,16]{1,2,0:T(8,128)(2,1)S(1)}, u32[]{:S(2)}, u32[]{:S(2)}) async-start(bf16[4,512,16]{1,2,0:T(8,128)(2,1)} %stack.2), calls=%async_computation.2 | async-start | bytes 131072 | tf_op jit(solution)/shard_map/all_to_all | solution.py:31
  89.3 369.8 %all-to-all-start.1 = ((bf16[16,512,1024]{1,0,2:T(8,128)(2,1)}), bf16[16,512,1024]{1,0,2:T(8,128)(2,1)}, u32[]{:S(2)}, u32[]{:S(2)}) async-start(bf16[16,512,1024]{1,0,2:T(8,128)(2,1)} %divide_convert_fusion), calls=%async_computation.1 | async-start | bytes 33554432 | tf_op jit(solution)/shard_map/all_to_all | solution.py:21
  96.4 34.2 %copy-start = (f32[16,1024]{1,0:T(8,128)S(1)}, f32[16,1024]{1,0:T(8,128)}, u32[]{:S(2)}) copy-start(f32[16,1024]{1,0:T(8,128)} %get-tuple-element.5) | copy-start | bytes 196612
  459.2 369.4 %all-to-all-start = ((bf16[16,512,1024]{1,0,2:T(8,128)(2,1)}), bf16[16,512,1024]{1,0,2:T(8,128)(2,1)}, u32[]{:S(2)}, u32[]{:S(2)}) async-start(bf16[16,512,1024]{1,0,2:T(8,128)(2,1)} %divide_convert_fusion.1), calls=%async_computation | async-start | bytes 33554432 | tf_op jit(solution)/shard_map/all_to_all | solution.py:20
Sparse Core Ops, SparseCore 0:
  29.5 37.5 all-reduce.2
